TPU v7x, 32 devices: a whole 2x2x4 slice. The times are simulated.
32 devices in a mesh: seq: 8 (over z, y), head: 4 (over x, core).
Axes of the slice: x: 2, y: 2, z: 4, core: 2. Of those that a mesh axis runs over, the one named last changes fastest.
Arguments:
- image_patches: bfloat16 [8, 256, 1152], P('seq', None, 'head'), may hold values from -6 to 6
- text_embed: bfloat16 [2048, 2048], P('seq', 'head'), may hold values from -6 to 6
- image_start: int32 [8], replicated, may hold values from 0 to 30, as said below
- image_forget: float32 [8], replicated, may hold values from 0.001 to 0.3
- adapter: bfloat16 [1152, 2048], P('head'), may hold values from -0.1875 to 0.1875
- norm_gain: float32 [2048], replicated, may hold values from 0.5 to 1.5
- in_proj: bfloat16 [2048, 4, 2048], P(None, None, 'head'), may hold values from -0.125 to 0.125
- decay_proj: bfloat16 [2048, 16], P(None, 'head'), may hold values from -0.125 to 0.125
- head_decay_ceiling: float32 [16], P('head'), may hold values from 0 to 1, as said below
- out_gain: float32 [16, 128], P('head'), may hold values from 0.5 to 1.5
- out_proj: bfloat16 [2048, 2048], P('head'), may hold values from -0.125 to 0.125
Outputs:
- image_out: bfloat16 [8, 256, 2048], P('seq', None, 'head')
- text_out: bfloat16 [2048, 2048], P('seq', 'head')
Inputs may be any that keep to these rules, and one draw needn't show every extreme that they name: `image_start`: each entry is even; the images take distinct pairs of blocks. The merged piece of 512 tokens on one device of seq never holds both the image and the text that one device of seq holds in the source layout. `head_decay_ceiling`: Positive.
All inputs are finite; a program needn't handle non-finite values.
Results may differ from a plain program's by a relative error of at most 0.0095.
Values may be sent and summed in bfloat16 or wider, within the bound.
A program may use at most 128 MiB of HBM per device.

v0:
```python
import jax
import jax.numpy as jnp
from jax import lax
from jax.sharding import PartitionSpec as P

EPSILON = 1e-06


def prefix(array, axis, join, neutral):
    place = lax.axis_index(axis)
    gathered = jax.tree.map(
        lambda a, kind: lax.all_gather(a.astype(kind), axis), array, (jnp.bfloat16, jnp.bfloat16)
    )
    state = jax.tree.map(lambda a, e: jnp.zeros_like(a) + jnp.asarray(e, a.dtype), array, neutral)

    def one(step, state):
        return join(
            state,
            jax.tree.map(
                lambda a, own: lax.dynamic_index_in_dim(a, step, 0, False).astype(own.dtype),
                gathered,
                array,
            ),
        )

    return lax.fori_loop(0, place, one, state)


def rms_scale(values, gain_row):
    mean_square = jnp.mean(values * values, axis=-1, keepdims=True)
    return values * lax.rsqrt(mean_square + EPSILON) * gain_row


def shards(
    image_patches,
    text_embed,
    image_start,
    image_forget,
    adapter,
    norm_gain,
    in_proj,
    decay_proj,
    head_decay_ceiling,
    out_gain,
    out_proj,
):
    seq_count = lax.axis_size("seq")
    my_index = lax.axis_index("seq")
    patch_row_block = text_embed.shape[0]
    local_width = text_embed.shape[1]
    share_rows = patch_row_block // seq_count
    unit_count = 2 * seq_count
    token_rows = 2 * patch_row_block
    unit_ids = jnp.arange(unit_count, dtype=jnp.int32)
    device_ids = jnp.arange(seq_count, dtype=jnp.int32)
    unit_of_image = image_start // 2
    image_hits = (unit_of_image[:, None] == unit_ids[None, :]).astype(jnp.int32)
    is_image = jnp.sum(image_hits, axis=0)
    image_here = jnp.sum(image_hits * device_ids[:, None], axis=0)
    is_text = 1 - is_image
    text_here = jnp.cumsum(is_text) - is_text
    text_pick = ((is_text[None, :] == 1) & (text_here[None, :] == device_ids[:, None])).astype(
        jnp.int32
    )
    text_unit = jnp.sum(text_pick * unit_ids[None, :], axis=1)
    source = jnp.where(is_image == 1, image_here, text_here)
    my_units = 2 * my_index + jnp.arange(2, dtype=jnp.int32)
    unit_image = jnp.take(is_image, my_units)
    partial_value = jnp.dot(image_patches[0], adapter, preferred_element_type=jnp.float32)
    embedded = lax.psum_scatter(partial_value, "head", scatter_dimension=1, tiled=True).astype(
        jnp.bfloat16
    )
    units_here = jnp.stack([embedded, text_embed]).reshape(2, seq_count, share_rows, local_width)
    spread = lax.all_to_all(units_here, "seq", split_axis=1, concat_axis=1, tiled=True)
    table = spread.reshape(unit_count, share_rows, local_width)
    pick_index = is_text * seq_count + source
    outgoing_units = jnp.take(table, pick_index, axis=0).reshape(
        seq_count, 2, share_rows, local_width
    )
    arrived = lax.all_to_all(outgoing_units, "seq", split_axis=0, concat_axis=2, tiled=True)
    merged = arrived.reshape(token_rows, local_width)
    full_rows = lax.all_gather(merged, "head", axis=1, tiled=True)
    normed = rms_scale(full_rows.astype(jnp.float32), norm_gain).astype(jnp.bfloat16)
    model_width = in_proj.shape[0]
    head_count = head_decay_ceiling.shape[0]
    head_width = out_gain.shape[1]
    projected = jnp.dot(
        normed, in_proj.reshape(model_width, -1), preferred_element_type=jnp.float32
    )
    projected = projected.astype(jnp.bfloat16).reshape(token_rows, 4, head_count, head_width)
    gate_preactivation = jnp.dot(normed, decay_proj, preferred_element_type=jnp.float32)
    forget_element = jnp.where(
        unit_image == 1, jnp.log1p(-jnp.take(image_forget, jnp.take(image_here, my_units))), 0.0
    )
    start_offsets = jnp.arange(token_rows, dtype=jnp.int32) % patch_row_block == 0
    surge_logarithm = jnp.where(start_offsets, jnp.repeat(forget_element, patch_row_block), 0.0)
    decay_logarithm = (
        -head_decay_ceiling[None, :] * jax.nn.sigmoid(gate_preactivation) + surge_logarithm[:, None]
    )
    queries = projected[:, 0]
    key_rows = projected[:, 1]
    value_rows = projected[:, 2]
    gate_rows = projected[:, 3]
    within = jnp.cumsum(decay_logarithm, axis=0)
    span_decay = within[-1]
    scores = jnp.einsum("thd,shd->hts", queries, key_rows, preferred_element_type=jnp.float32)
    lagged = within.T[:, :, None] - within.T[:, None, :]
    row_ids = jnp.arange(token_rows, dtype=jnp.int32)
    causal = (row_ids[:, None] >= row_ids[None, :])[None]
    weights = jnp.where(causal, scores * jnp.exp(jnp.where(causal, lagged, 0.0)), 0.0).astype(
        jnp.bfloat16
    )
    inner_part = jnp.einsum("hts,shd->thd", weights, value_rows, preferred_element_type=jnp.float32)
    weighted_keys = key_rows.astype(jnp.float32) * jnp.exp(span_decay[None, :] - within)[:, :, None]
    local_state = jnp.einsum(
        "thd,the->hde",
        weighted_keys,
        value_rows.astype(jnp.float32),
        precision=lax.Precision.HIGHEST,
    )

    def combine(earlier, later_part):
        return (
            earlier[0] + later_part[0],
            jnp.exp(later_part[0])[:, None, None] * earlier[1] + later_part[1],
        )

    identity = (jnp.zeros_like(span_decay), jnp.zeros_like(local_state))
    decay_before, entering = prefix((span_decay, local_state), "seq", combine, identity)
    carried = jnp.exp(within)[:, :, None] * jnp.einsum(
        "thd,hde->the", queries.astype(jnp.float32), entering, precision=lax.Precision.HIGHEST
    )
    attended = inner_part + carried
    gated = rms_scale(attended, out_gain) * jax.nn.silu(gate_rows.astype(jnp.float32))
    gated = gated.astype(jnp.bfloat16).reshape(token_rows, -1)
    partial_out = jnp.dot(gated, out_proj, preferred_element_type=jnp.float32)
    summed = lax.psum_scatter(
        partial_out.astype(jnp.bfloat16), "head", scatter_dimension=1, tiled=True
    ).astype(jnp.float32)
    result = (merged.astype(jnp.float32) + summed).astype(jnp.bfloat16)
    result_shares = result.reshape(2, seq_count, share_rows, local_width)
    back_spread = lax.all_to_all(result_shares, "seq", split_axis=1, concat_axis=1, tiled=True)
    back_table = back_spread.reshape(unit_count, share_rows, local_width)
    wanted = jnp.stack([unit_of_image, text_unit], axis=1).reshape(-1)
    back_index = wanted % 2 * seq_count + wanted // 2
    outgoing = jnp.take(back_table, back_index, axis=0).reshape(
        seq_count, 2, share_rows, local_width
    )
    returned = lax.all_to_all(outgoing, "seq", split_axis=0, concat_axis=2, tiled=True)
    image_out = returned[:, 0]
    text_out = returned[0, 1]
    return (image_out, text_out)


def solution(mesh):
    in_specs = (
        P("seq", None, "head"),
        P("seq", "head"),
        P(),
        P(),
        P("head", None),
        P(),
        P(None, None, "head"),
        P(None, "head"),
        P("head"),
        P("head", None),
        P("head", None),
    )
    out_specs = (P("seq", None, "head"), P("seq", "head"))
    return jax.shard_map(shards, mesh=mesh, in_specs=in_specs, out_specs=out_specs, check_vma=False)
```

profile of v0, /device:TPU:0, one launch (start us, length us, event | category | flops | bytes accessed | tf_op | source)
XLA Modules:
  0.0 266.6 jit_solution(11392097754306038656)
XLA Ops:
  7.2 3.6 %fusion.25 = f32[256,2048]{1,0:T(8,128)} fusion(bf16[288,2048]{1,0:T(8,128)(2,1)} %param.21, bf16[1,256,288]{1,2,0:T(8,128)(2,1)} %param.17), kind=kOutput, calls=%fused_computation.50 | convolution fusion | flops 301989888 | bytes 3424256 | tf_op jit(solution)/shard_map/dot_general | solution.py:69
  10.8 34.0 %reduce-scatter.3.cloned.1.call-done = f32[256,512]{1,0:T(8,128)} async-done(((f32[256,2048]{1,0:T(8,128)}), f32[256,512]{1,0:T(8,128)}) %reduce-scatter.3.cloned.1.call-update) | async-done | bytes 524304 | tf_op jit(solution)/shard_map/reduce_scatter | solution.py:70
  44.9 1.1 convert_element_type.68
  46.0 0.8 pad_maximum_fusion
  46.8 5.6 %all-to-all-start = ((bf16[2,8,32,512]{3,2,0,1:T(8,128)(2,1)}), bf16[2,8,32,512]{3,2,0,1:T(8,128)(2,1)S(1)}, u32[]{:S(2)}, u32[]{:S(2)}) async-start(bf16[2,8,32,512]{3,2,0,1:T(8,128)(2,1)} %pad_maximum_fusion), calls=%async_computation.1 | async-start | bytes 1048576 | tf_op jit(solution)/shard_map/all_to_all | solution.py:74
  52.9 13.9 %all-to-all-done = bf16[2,8,32,512]{3,2,0,1:T(8,128)(2,1)S(1)} async-done(((bf16[2,8,32,512]{3,2,0,1:T(8,128)(2,1)}), bf16[2,8,32,512]{3,2,0,1:T(8,128)(2,1)S(1)}, u32[]{:S(2)}, u32[]{:S(2)}) %all-to-all-start) | async-done | bytes 524320 | tf_op jit(solution)/shard_map/all_to_all | solution.py:74
  67.6 18.0 %all_to_all.43 = bf16[8,2,32,512]{3,2,1,0:T(8,128)(2,1)S(1)} all-to-all(bf16[8,2,32,512]{3,2,1,0:T(8,128)(2,1)S(1)} %bitcast.109), channel_id=1, replica_groups=mesh['seq'=8,'head'=4] {'seq'}, dimensions={0} | all-to-all | bytes 1048576 | tf_op jit(solution)/shard_map/all_to_all | solution.py:80
  85.6 0.9 copy.135
  87.2 0.6 gather_fusion.2
  88.6 10.6 %copy.155 = bf16[256,8,4,512]{3,1,2,0:T(8,128)(2,1)} copy(bf16[256,8,4,512]{3,2,1,0:T(4,128)(2,1)} %bitcast.103) | data formatting | bytes 16777216
  99.2 8.1 %all-gather.5.cloned.1.call-done = bf16[512,2048]{1,0:T(8,128)(2,1)} async-done(((bf16[512,512]{1,0:T(8,128)(2,1)}), bf16[512,2048]{1,0:T(8,128)(2,1)}) %all-gather.5.cloned.1.call-update) | async-done | bytes 2097168 | tf_op jit(solution)/shard_map/all_gather | solution.py:82
  107.3 2.1 fusion
  109.4 2.3 fusion.12
  111.8 1.2 reduce-window.18
  113.7 9.9 %convolution_convert_fusion.1 = bf16[512,2048]{1,0:T(8,128)(2,1)} fusion(bf16[2048,2048]{1,0:T(8,128)(2,1)} %bitcast.104, bf16[512,2048]{1,0:T(8,128)(2,1)} %all-gather.5.cloned.1.call-done, f32[2048]{0:T(1024)S(1)} %copy-done.7, f32[512]{0:T(512)S(1)} %add_rsqrt_fusion.1), kind=kOutput, calls=%fused_computation.14 | convolution fusion | flops 4300210176 | bytes 12593152 | tf_op jit(solution)/shard_map/dot_general | solution.py:87
  123.5 4.4 %reshape.189 = bf16[512,4,4,128]{3,2,1,0:T(4,128)(2,1)} reshape(bf16[512,2048]{1,0:T(8,128)(2,1)} %convolution_convert_fusion.1) | data formatting | bytes 4194304 | tf_op jit(solution)/shard_map/reshape | solution.py:90
  128.0 3.2 %fusion.41 = (bf16[512,1,4,128]{3,2,1,0:T(4,128)(2,1)S(1)}, bf16[512,1,4,128]{3,2,1,0:T(4,128)(2,1)}, bf16[512,1,4,128]{3,2,1,0:T(4,128)(2,1)S(1)}, bf16[512,1,4,128]{3,2,1,0:T(4,128)(2,1)}) fusion(bf16[512,4,4,128]{3,2,1,0:T(4,128)(2,1)} %reshape.189), kind=kLoop, calls=%fused_computation.109 | loop fusion | bytes 4194304 | tf_op jit(solution)/shard_map/slice | solution.py:103
  131.2 1.1 copy.151
  132.3 3.2 %convolution_convert_fusion.2 = bf16[4,128,128]{2,1,0:T(8,128)(2,1)} fusion(bf16[512,1,4,128]{0,3,2,1:T(8,128)(2,1)} %copy.151, f32[512,4]{0,1:T(4,128)S(1)} %get-tuple-element.112, bf16[512,1,4,128]{3,2,1,0:T(4,128)(2,1)} %get-tuple-element.108), kind=kOutput, calls=%fused_computation.22 | convolution fusion | flops 403243008 | bytes 1187840 | tf_op jit(solution)/shard_map/thd,the->hde/dot_general | solution.py:115
  135.6 0.8 iota_compare_fusion
  136.5 20.7 %all-gather.1 = bf16[8,1,4]{2,1,0:T(2,128)(2,1)S(1)} all-gather(bf16[1,1,4]{2,1,0:T(2,128)(2,1)S(1)} %bitcast.124), channel_id=1, replica_groups=mesh['seq'=8,'head'=4] {'seq'}, dimensions={0}, use_global_device_ids=true | all-gather | bytes 72 | tf_op jit(solution)/shard_map/all_gather | solution.py:12
  157.7 4.4 %fusion.4 = f32[512,4,128]{0,2,1:T(8,128)} fusion(f32[4,512]{1,0:T(4,128)S(1)} %bitcast.120, pred[512,512]{1,0:T(8,128)(4,1)} %iota_compare_fusion, bf16[512,1,4,128]{0,3,2,1:T(8,128)(2,1)} %copy.151, bf16[512,1,4,128]{3,2,1,0:T(4,128)(2,1)} %get-tuple-element.106, bf16[512,1,4,128]{3,2,1,0:T(4,128)(2,1)} %get-tuple-element.108), kind=kOutput, calls=%fused_computation.16 | convolution fusion | flops 542113792 | bytes 2891776 | tf_op jit(solution)/shard_map/hts,shd->thd/dot_general | solution.py:113
  162.1 13.9 %all-gather.7.cloned.1.call-done = bf16[32,128,128]{2,1,0:T(8,128)(2,1)} async-done(((bf16[4,128,128]{2,1,0:T(8,128)(2,1)}), bf16[32,128,128]{2,1,0:T(8,128)(2,1)}) %all-gather.7.cloned.1.call-update) | async-done | bytes 1048592 | tf_op jit(solution)/shard_map/all_gather | solution.py:12
  176.1 2.0 multiply_reduce_fusion
  178.4 2.6 convolution_convert_fusion
  181.1 37.5 %reduce-scatter.5.cloned.1.call-done = bf16[512,512]{1,0:T(8,128)(2,1)} async-done(((bf16[512,2048]{1,0:T(8,128)(2,1)}), bf16[512,512]{1,0:T(8,128)(2,1)}) %reduce-scatter.5.cloned.1.call-update) | async-done | bytes 524304 | tf_op jit(solution)/shard_map/reduce_scatter | solution.py:137
  218.6 1.2 add_convert_fusion
  219.8 0.8 copy.145
  220.6 5.5 %all-to-all-start.2 = ((bf16[2,8,32,512]{3,2,0,1:T(8,128)(2,1)}), bf16[2,8,32,512]{3,2,0,1:T(8,128)(2,1)S(1)}, u32[]{:S(2)}, u32[]{:S(2)}) async-start(bf16[2,8,32,512]{3,2,0,1:T(8,128)(2,1)} %copy.145), calls=%async_computation.4 | async-start | bytes 1048576 | tf_op jit(solution)/shard_map/all_to_all | solution.py:142
  226.5 14.0 %all-to-all-done.2 = bf16[2,8,32,512]{3,2,0,1:T(8,128)(2,1)S(1)} async-done(((bf16[2,8,32,512]{3,2,0,1:T(8,128)(2,1)}), bf16[2,8,32,512]{3,2,0,1:T(8,128)(2,1)S(1)}, u32[]{:S(2)}, u32[]{:S(2)}) %all-to-all-start.2) | async-done | bytes 524320 | tf_op jit(solution)/shard_map/all_to_all | solution.py:142
  241.2 18.0 %all_to_all.44 = bf16[8,2,32,512]{3,2,1,0:T(8,128)(2,1)S(1)} all-to-all(bf16[8,2,32,512]{3,2,1,0:T(8,128)(2,1)S(1)} %bitcast.111), channel_id=1, replica_groups=mesh['seq'=8,'head'=4] {'seq'}, dimensions={0} | all-to-all | bytes 1048576 | tf_op jit(solution)/shard_map/all_to_all | solution.py:149
  259.3 0.8 slice_bitcast_fusion
  (78 shorter events, 5.7 us)
Async XLA Ops:
  7.2 171.3 %copy-start = (bf16[512,2048]{1,0:T(8,128)(2,1)S(1)}, bf16[512,2048]{1,0:T(8,128)(2,1)}, u32[]{:S(2)}) copy-start(bf16[512,2048]{1,0:T(8,128)(2,1)} %param.27) | copy-start | bytes 6291460
  7.2 38.8 %copy-start.4 = (bf16[256,512]{1,0:T(8,128)(2,1)S(1)}, bf16[256,512]{1,0:T(8,128)(2,1)}, u32[]{:S(2)}) copy-start(bf16[256,512]{1,0:T(8,128)(2,1)} %param.18) | copy-start | bytes 786436
  7.2 45.3 %copy-start.9 = (s32[8]{0:T(128)S(1)}, s32[8]{0:T(128)}, u32[]{:S(2)}) copy-start(s32[8]{0:T(128)} %param.19) | copy-start | bytes 100
  7.2 37.7 %reduce-scatter.3.cloned.1.call-start = ((), (), s32[]{:S(2)}) async-start(), calls=%async_computation.6 | async-start | bytes 2621440 | tf_op jit(solution)/shard_map/reduce_scatter | solution.py:70
  46.8 41.0 %copy-start.1 = (f32[8]{0:T(128)S(1)}, f32[8]{0:T(128)}, u32[]{:S(2)}) copy-start(f32[8]{0:T(128)} %param.20) | copy-start | bytes 100
  46.8 41.8 %copy-start.8 = (f32[4]{0:T(128)S(1)}, f32[4]{0:T(128)}, u32[]{:S(2)}) copy-start(f32[4]{0:T(128)} %param.25) | copy-start | bytes 52
  46.8 20.0 %all-to-all-start = ((bf16[2,8,32,512]{3,2,0,1:T(8,128)(2,1)}), bf16[2,8,32,512]{3,2,0,1:T(8,128)(2,1)S(1)}, u32[]{:S(2)}, u32[]{:S(2)}) async-start(bf16[2,8,32,512]{3,2,0,1:T(8,128)(2,1)} %pad_maximum_fusion), calls=%async_computation.1 | async-start | bytes 1048576 | tf_op jit(solution)/shard_map/all_to_all | solution.py:74
  52.5 54.8 %all-gather.5.cloned.1.call-start = ((), (), s32[]{:S(2)}) async-start(), calls=%async_computation.7 | async-start | bytes 2621440 | tf_op jit(solution)/shard_map/all_gather | solution.py:82
  86.5 89.5 %all-gather.7.cloned.1.call-start = ((), (), s32[]{:S(2)}) async-start(), calls=%async_computation.9 | async-start | bytes 1179648 | tf_op jit(solution)/shard_map/all_gather | solution.py:12
  88.6 20.8 %copy-start.6 = (bf16[2048,4]{0,1:T(4,128)(2,1)S(1)}, bf16[2048,4]{0,1:T(4,128)(2,1)}, u32[]{:S(2)}) copy-start(bf16[2048,4]{0,1:T(4,128)(2,1)} %param.24) | copy-start | bytes 49156
  88.6 20.8 %copy-start.7 = (f32[2048]{0:T(1024)S(1)}, f32[2048]{0:T(1024)}, u32[]{:S(2)}) copy-start(f32[2048]{0:T(1024)} %param.22) | copy-start | bytes 24580
  135.5 83.1 %reduce-scatter.5.cloned.1.call-start = ((), (), s32[]{:S(2)}) async-start(), calls=%async_computation.8 | async-start | bytes 2621440 | tf_op jit(solution)/shard_map/reduce_scatter | solution.py:137
  157.7 18.3 %copy-start.3 = (bf16[512,1,4,128]{3,2,1,0:T(4,128)(2,1)S(1)}, bf16[512,1,4,128]{3,2,1,0:T(4,128)(2,1)}, u32[]{:S(2)}) copy-start(bf16[512,1,4,128]{3,2,1,0:T(4,128)(2,1)} %get-tuple-element.106) | copy-start | bytes 1572868
  162.1 15.9 %copy-start.5 = (f32[4,128]{1,0:T(4,128)S(1)}, f32[4,128]{1,0:T(4,128)}, u32[]{:S(2)}) copy-start(f32[4,128]{1,0:T(4,128)} %param.26) | copy-start | bytes 6148
  178.4 40.2 %copy-start.2 = (bf16[1,2,8,32,512]{4,3,2,1,0:T(8,128)(2,1)S(1)}, bf16[1,2,8,32,512]{4,3,2,1,0:T(8,128)(2,1)}, u32[]{:S(2)}) copy-start(bf16[1,2,8,32,512]{4,3,2,1,0:T(8,128)(2,1)} %copy.135) | copy-start | bytes 1572868
  220.6 19.8 %all-to-all-start.2 = ((bf16[2,8,32,512]{3,2,0,1:T(8,128)(2,1)}), bf16[2,8,32,512]{3,2,0,1:T(8,128)(2,1)S(1)}, u32[]{:S(2)}, u32[]{:S(2)}) async-start(bf16[2,8,32,512]{3,2,0,1:T(8,128)(2,1)} %copy.145), calls=%async_computation.4 | async-start | bytes 1048576 | tf_op jit(solution)/shard_map/all_to_all | solution.py:142
Sparse Core Ops, SparseCore 0:
  11.0 33.8 reduce-scatter.2
  86.6 20.6 all-gather.4
  135.6 40.3 all-gather.6
  181.2 37.2 reduce-scatter.4
where the time goes:
time: 267 us
  waiting for transfers between devices  121 us (45%)
  blocking collectives  56.7 us (21%)
  matrix products  27.9 us (10%)
  local copies, waits for them, and re-layouts  26.5 us (10%)
  between operations  14.1 us (5%)
  starting transfers between devices  11.3 us (4%)
  other arithmetic  8.62 us (3%)
    reduce_scatter x1, waiting for transfers between devices, shards(): lax.psum_scatter(partial_out.astype(jnp.bfloat16), 'head', scatter_dimens...  37.5 us
    reduce_scatter x1, waiting for transfers between devices, shards(): lax.psum_scatter(partial_value, 'head', scatter_dimension=1, tiled=True)  34 us
    all_gather x1, blocking collectives, prefix(): lax.all_gather(a.astype(kind), axis)  20.7 us
    all_to_all x1, blocking collectives, shards(): lax.all_to_all(outgoing_units, 'seq', split_axis=0, concat_axis=2, tiled=...  18 us
    all_to_all x1, blocking collectives, shards(): lax.all_to_all(outgoing, 'seq', split_axis=0, concat_axis=2, tiled=True)  18 us
    all_to_all x1, waiting for transfers between devices, shards(): lax.all_to_all(result_shares, 'seq', split_axis=1, concat_axis=1, tiled=T...  14 us
    all_to_all x1, waiting for transfers between devices, shards(): lax.all_to_all(units_here, 'seq', split_axis=1, concat_axis=1, tiled=True)  13.9 us
    all_gather x1, waiting for transfers between devices, prefix(): lax.all_gather(a.astype(kind), axis)  13.9 us
  transfers between devices with their start and end apart: 6, of which 6 were waited for; matrix products, arithmetic and copies ran while one was open for 7% of the time, Pallas kernels for 0%

commit v1 on v0

--- a/solution.py
+++ b/solution.py
@@ -139,7 +139,12 @@
     ).astype(jnp.float32)
     result = (merged.astype(jnp.float32) + summed).astype(jnp.bfloat16)
     result_shares = result.reshape(2, seq_count, share_rows, local_width)
-    back_spread = lax.all_to_all(result_shares, "seq", split_axis=1, concat_axis=1, tiled=True)
+    back_spread = jnp.concatenate(
+        lax.all_to_all(
+            jnp.stack(jnp.split(result_shares, lax.axis_size("seq"), axis=1)), "seq", 0, 0
+        ),
+        axis=1,
+    )
     back_table = back_spread.reshape(unit_count, share_rows, local_width)
     wanted = jnp.stack([unit_of_image, text_unit], axis=1).reshape(-1)
     back_index = wanted % 2 * seq_count + wanted // 2

time: 267 us -> 272 us (1.019)
  local copies, waits for them, and re-layouts: 26.5 us -> 30.6 us
    unnamed x26 -> x33, local copies, waits for them, and re-layouts: 12.1 us -> 16.5 us
where the time goes in v1:
time: 272 us; the launch traced here: 271 us
  waiting for transfers between devices  121 us (44%)
  blocking collectives  56.7 us (21%)
  local copies, waits for them, and re-layouts  30.6 us (11%)
  matrix products  27.9 us (10%)
  between operations  14.1 us (5%)
  starting transfers between devices  11.3 us (4%)
  other arithmetic  8.63 us (3%)
    reduce_scatter x1, waiting for transfers between devices, shards(): lax.psum_scatter(partial_out.astype(jnp.bfloat16), 'head', scatter_dimens...  37.5 us
    reduce_scatter x1, waiting for transfers between devices, shards(): lax.psum_scatter(partial_value, 'head', scatter_dimension=1, tiled=True)  34 us
    all_gather x1, blocking collectives, prefix(): lax.all_gather(a.astype(kind), axis)  20.7 us
    all_to_all x1, blocking collectives, shards(): lax.all_to_all(outgoing_units, 'seq', split_axis=0, concat_axis=2, tiled=...  18 us
    all_to_all x1, blocking collectives, shards(): lax.all_to_all(outgoing, 'seq', split_axis=0, concat_axis=2, tiled=True)  18 us
    unnamed x33, local copies, waits for them, and re-layouts  16.5 us
    all_to_all x1, waiting for transfers between devices, shards(): lax.all_to_all(jnp.stack(jnp.split(result_shares, lax.axis_size('seq'), a...  14 us
    all_to_all x1, waiting for transfers between devices, shards(): lax.all_to_all(units_here, 'seq', split_axis=1, concat_axis=1, tiled=True)  13.9 us
  transfers between devices with their start and end apart: 6, of which 6 were waited for; matrix products, arithmetic and copies ran while one was open for 7% of the time, Pallas kernels for 0%

profile of v1, /device:TPU:0, one launch (start us, length us, event | category | flops | bytes accessed | tf_op | source)
XLA Modules:
  0.0 270.8 jit_solution(12812521529179281891)
XLA Ops:
  7.2 3.6 %fusion.25 = f32[256,2048]{1,0:T(8,128)} fusion(bf16[288,2048]{1,0:T(8,128)(2,1)} %param.21, bf16[1,256,288]{1,2,0:T(8,128)(2,1)} %param.17), kind=kOutput, calls=%fused_computation.50 | convolution fusion | flops 301989888 | bytes 3424256 | tf_op jit(solution)/shard_map/dot_general | solution.py:69
  10.8 34.0 %reduce-scatter.3.cloned.1.call-done = f32[256,512]{1,0:T(8,128)} async-done(((f32[256,2048]{1,0:T(8,128)}), f32[256,512]{1,0:T(8,128)}) %reduce-scatter.3.cloned.1.call-update) | async-done | bytes 524304 | tf_op jit(solution)/shard_map/reduce_scatter | solution.py:70
  44.9 1.1 convert_element_type.68
  46.0 0.8 pad_maximum_fusion
  46.8 5.6 %all-to-all-start = ((bf16[2,8,32,512]{3,2,0,1:T(8,128)(2,1)}), bf16[2,8,32,512]{3,2,0,1:T(8,128)(2,1)S(1)}, u32[]{:S(2)}, u32[]{:S(2)}) async-start(bf16[2,8,32,512]{3,2,0,1:T(8,128)(2,1)} %pad_maximum_fusion), calls=%async_computation.1 | async-start | bytes 1048576 | tf_op jit(solution)/shard_map/all_to_all | solution.py:74
  52.9 13.9 %all-to-all-done = bf16[2,8,32,512]{3,2,0,1:T(8,128)(2,1)S(1)} async-done(((bf16[2,8,32,512]{3,2,0,1:T(8,128)(2,1)}), bf16[2,8,32,512]{3,2,0,1:T(8,128)(2,1)S(1)}, u32[]{:S(2)}, u32[]{:S(2)}) %all-to-all-start) | async-done | bytes 524320 | tf_op jit(solution)/shard_map/all_to_all | solution.py:74
  67.6 18.0 %all_to_all.43 = bf16[8,2,32,512]{3,2,1,0:T(8,128)(2,1)S(1)} all-to-all(bf16[8,2,32,512]{3,2,1,0:T(8,128)(2,1)S(1)} %bitcast.166), channel_id=1, replica_groups=mesh['seq'=8,'head'=4] {'seq'}, dimensions={0} | all-to-all | bytes 1048576 | tf_op jit(solution)/shard_map/all_to_all | solution.py:80
  85.6 0.9 copy.187
  86.6 0.6 gather_fusion.3
  87.2 0.6 gather_fusion.2
  88.6 10.6 %copy.222 = bf16[256,8,4,512]{3,1,2,0:T(8,128)(2,1)} copy(bf16[256,8,4,512]{3,2,1,0:T(4,128)(2,1)} %bitcast.153) | data formatting | bytes 16777216
  99.2 8.1 %all-gather.5.cloned.1.call-done = bf16[512,2048]{1,0:T(8,128)(2,1)} async-done(((bf16[512,512]{1,0:T(8,128)(2,1)}), bf16[512,2048]{1,0:T(8,128)(2,1)}) %all-gather.5.cloned.1.call-update) | async-done | bytes 2097168 | tf_op jit(solution)/shard_map/all_gather | solution.py:82
  107.3 2.1 fusion
  109.4 2.3 fusion.12
  111.8 1.2 reduce-window.18
  113.7 9.9 %convolution_convert_fusion.1 = bf16[512,2048]{1,0:T(8,128)(2,1)} fusion(bf16[2048,2048]{1,0:T(8,128)(2,1)} %bitcast.154, bf16[512,2048]{1,0:T(8,128)(2,1)} %all-gather.5.cloned.1.call-done, f32[2048]{0:T(1024)S(1)} %copy-done.7, f32[512]{0:T(512)S(1)} %add_rsqrt_fusion.1), kind=kOutput, calls=%fused_computation.14 | convolution fusion | flops 4300210176 | bytes 12593152 | tf_op jit(solution)/shard_map/dot_general | solution.py:87
  123.6 4.4 %reshape.189 = bf16[512,4,4,128]{3,2,1,0:T(4,128)(2,1)} reshape(bf16[512,2048]{1,0:T(8,128)(2,1)} %convolution_convert_fusion.1) | data formatting | bytes 4194304 | tf_op jit(solution)/shard_map/reshape | solution.py:90
  128.0 3.2 %fusion.49 = (bf16[512,1,4,128]{3,2,1,0:T(4,128)(2,1)S(1)}, bf16[512,1,4,128]{3,2,1,0:T(4,128)(2,1)}, bf16[512,1,4,128]{3,2,1,0:T(4,128)(2,1)S(1)}, bf16[512,1,4,128]{3,2,1,0:T(4,128)(2,1)}) fusion(bf16[512,4,4,128]{3,2,1,0:T(4,128)(2,1)} %reshape.189), kind=kLoop, calls=%fused_computation.125 | loop fusion | bytes 4194304 | tf_op jit(solution)/shard_map/slice | solution.py:103
  131.2 1.1 copy.210
  132.3 3.2 %convolution_convert_fusion.2 = bf16[4,128,128]{2,1,0:T(8,128)(2,1)} fusion(bf16[512,1,4,128]{0,3,2,1:T(8,128)(2,1)} %copy.210, f32[512,4]{0,1:T(4,128)S(1)} %get-tuple-element.112, bf16[512,1,4,128]{3,2,1,0:T(4,128)(2,1)} %get-tuple-element.108), kind=kOutput, calls=%fused_computation.22 | convolution fusion | flops 403243008 | bytes 1187840 | tf_op jit(solution)/shard_map/thd,the->hde/dot_general | solution.py:115
  135.6 0.8 iota_compare_fusion
  136.5 20.7 %all-gather.1 = bf16[8,1,4]{2,1,0:T(2,128)(2,1)S(1)} all-gather(bf16[1,1,4]{2,1,0:T(2,128)(2,1)S(1)} %bitcast.181), channel_id=1, replica_groups=mesh['seq'=8,'head'=4] {'seq'}, dimensions={0}, use_global_device_ids=true | all-gather | bytes 72 | tf_op jit(solution)/shard_map/all_gather | solution.py:12
  157.8 4.4 %fusion.4 = f32[512,4,128]{0,2,1:T(8,128)} fusion(f32[4,512]{1,0:T(4,128)S(1)} %bitcast.177, pred[512,512]{1,0:T(8,128)(4,1)} %iota_compare_fusion, bf16[512,1,4,128]{0,3,2,1:T(8,128)(2,1)} %copy.210, bf16[512,1,4,128]{3,2,1,0:T(4,128)(2,1)} %get-tuple-element.106, bf16[512,1,4,128]{3,2,1,0:T(4,128)(2,1)} %get-tuple-element.108), kind=kOutput, calls=%fused_computation.16 | convolution fusion | flops 542113792 | bytes 2891776 | tf_op jit(solution)/shard_map/hts,shd->thd/dot_general | solution.py:113
  162.2 13.8 %all-gather.7.cloned.1.call-done = bf16[32,128,128]{2,1,0:T(8,128)(2,1)} async-done(((bf16[4,128,128]{2,1,0:T(8,128)(2,1)}), bf16[32,128,128]{2,1,0:T(8,128)(2,1)}) %all-gather.7.cloned.1.call-update) | async-done | bytes 1048592 | tf_op jit(solution)/shard_map/all_gather | solution.py:12
  176.0 2.0 multiply_reduce_fusion
  178.4 2.6 convolution_convert_fusion
  181.1 37.5 %reduce-scatter.5.cloned.1.call-done = bf16[512,512]{1,0:T(8,128)(2,1)} async-done(((bf16[512,2048]{1,0:T(8,128)(2,1)}), bf16[512,512]{1,0:T(8,128)(2,1)}) %reduce-scatter.5.cloned.1.call-update) | async-done | bytes 524304 | tf_op jit(solution)/shard_map/reduce_scatter | solution.py:137
  218.6 1.2 add_convert_fusion
  224.7 5.5 %all-to-all-start.2 = ((bf16[8,2,1,32,512]{4,3,1,2,0:T(8,128)(2,1)}), bf16[8,2,1,32,512]{4,3,1,2,0:T(8,128)(2,1)S(1)}, u32[]{:S(2)}, u32[]{:S(2)}) async-start(bf16[8,2,1,32,512]{4,3,1,2,0:T(8,128)(2,1)} %fusion.27), calls=%async_computation.4 | async-start | bytes 1048576 | tf_op jit(solution)/shard_map/all_to_all | solution.py:143
  230.6 14.0 %all-to-all-done.2 = bf16[8,2,1,32,512]{4,3,1,2,0:T(8,128)(2,1)S(1)} async-done(((bf16[8,2,1,32,512]{4,3,1,2,0:T(8,128)(2,1)}), bf16[8,2,1,32,512]{4,3,1,2,0:T(8,128)(2,1)S(1)}, u32[]{:S(2)}, u32[]{:S(2)}) %all-to-all-start.2) | async-done | bytes 524320 | tf_op jit(solution)/shard_map/all_to_all | solution.py:143
  245.3 18.0 %all_to_all.44 = bf16[8,2,32,512]{3,2,1,0:T(8,128)(2,1)S(1)} all-to-all(bf16[8,2,32,512]{3,2,1,0:T(8,128)(2,1)S(1)} %bitcast.168), channel_id=1, replica_groups=mesh['seq'=8,'head'=4] {'seq'}, dimensions={0} | all-to-all | bytes 1048576 | tf_op jit(solution)/shard_map/all_to_all | solution.py:154
  263.4 0.8 slice_bitcast_fusion
  (85 shorter events, 10.1 us)
Async XLA Ops:
  7.2 171.3 %copy-start = (bf16[512,2048]{1,0:T(8,128)(2,1)S(1)}, bf16[512,2048]{1,0:T(8,128)(2,1)}, u32[]{:S(2)}) copy-start(bf16[512,2048]{1,0:T(8,128)(2,1)} %param.27) | copy-start | bytes 6291460
  7.2 38.8 %copy-start.4 = (bf16[256,512]{1,0:T(8,128)(2,1)S(1)}, bf16[256,512]{1,0:T(8,128)(2,1)}, u32[]{:S(2)}) copy-start(bf16[256,512]{1,0:T(8,128)(2,1)} %param.18) | copy-start | bytes 786436
  7.2 45.3 %copy-start.9 = (s32[8]{0:T(128)S(1)}, s32[8]{0:T(128)}, u32[]{:S(2)}) copy-start(s32[8]{0:T(128)} %param.19) | copy-start | bytes 100
  7.2 37.7 %reduce-scatter.3.cloned.1.call-start = ((), (), s32[]{:S(2)}) async-start(), calls=%async_computation.6 | async-start | bytes 2621440 | tf_op jit(solution)/shard_map/reduce_scatter | solution.py:70
  46.8 41.0 %copy-start.1 = (f32[8]{0:T(128)S(1)}, f32[8]{0:T(128)}, u32[]{:S(2)}) copy-start(f32[8]{0:T(128)} %param.20) | copy-start | bytes 100
  46.8 41.8 %copy-start.8 = (f32[4]{0:T(128)S(1)}, f32[4]{0:T(128)}, u32[]{:S(2)}) copy-start(f32[4]{0:T(128)} %param.25) | copy-start | bytes 52
  46.8 20.0 %all-to-all-start = ((bf16[2,8,32,512]{3,2,0,1:T(8,128)(2,1)}), bf16[2,8,32,512]{3,2,0,1:T(8,128)(2,1)S(1)}, u32[]{:S(2)}, u32[]{:S(2)}) async-start(bf16[2,8,32,512]{3,2,0,1:T(8,128)(2,1)} %pad_maximum_fusion), calls=%async_computation.1 | async-start | bytes 1048576 | tf_op jit(solution)/shard_map/all_to_all | solution.py:74
  52.5 54.8 %all-gather.5.cloned.1.call-start = ((), (), s32[]{:S(2)}) async-start(), calls=%async_computation.7 | async-start | bytes 2621440 | tf_op jit(solution)/shard_map/all_gather | solution.py:82
  86.5 89.5 %all-gather.7.cloned.1.call-start = ((), (), s32[]{:S(2)}) async-start(), calls=%async_computation.9 | async-start | bytes 1179648 | tf_op jit(solution)/shard_map/all_gather | solution.py:12
  88.6 20.8 %copy-start.6 = (bf16[2048,4]{0,1:T(4,128)(2,1)S(1)}, bf16[2048,4]{0,1:T(4,128)(2,1)}, u32[]{:S(2)}) copy-start(bf16[2048,4]{0,1:T(4,128)(2,1)} %param.24) | copy-start | bytes 49156
  88.6 20.8 %copy-start.7 = (f32[2048]{0:T(1024)S(1)}, f32[2048]{0:T(1024)}, u32[]{:S(2)}) copy-start(f32[2048]{0:T(1024)} %param.22) | copy-start | bytes 24580
  135.5 83.0 %reduce-scatter.5.cloned.1.call-start = ((), (), s32[]{:S(2)}) async-start(), calls=%async_computation.8 | async-start | bytes 2621440 | tf_op jit(solution)/shard_map/reduce_scatter | solution.py:137
  157.7 18.3 %copy-start.3 = (bf16[512,1,4,128]{3,2,1,0:T(4,128)(2,1)S(1)}, bf16[512,1,4,128]{3,2,1,0:T(4,128)(2,1)}, u32[]{:S(2)}) copy-start(bf16[512,1,4,128]{3,2,1,0:T(4,128)(2,1)} %get-tuple-element.106) | copy-start | bytes 1572868
  162.2 15.9 %copy-start.5 = (f32[4,128]{1,0:T(4,128)S(1)}, f32[4,128]{1,0:T(4,128)}, u32[]{:S(2)}) copy-start(f32[4,128]{1,0:T(4,128)} %param.26) | copy-start | bytes 6148
  178.4 40.1 %copy-start.2 = (bf16[1,2,8,32,512]{4,3,2,1,0:T(8,128)(2,1)S(1)}, bf16[1,2,8,32,512]{4,3,2,1,0:T(8,128)(2,1)}, u32[]{:S(2)}) copy-start(bf16[1,2,8,32,512]{4,3,2,1,0:T(8,128)(2,1)} %copy.187) | copy-start | bytes 1572868
  224.7 19.8 %all-to-all-start.2 = ((bf16[8,2,1,32,512]{4,3,1,2,0:T(8,128)(2,1)}), bf16[8,2,1,32,512]{4,3,1,2,0:T(8,128)(2,1)S(1)}, u32[]{:S(2)}, u32[]{:S(2)}) async-start(bf16[8,2,1,32,512]{4,3,1,2,0:T(8,128)(2,1)} %fusion.27), calls=%async_computation.4 | async-start | bytes 1048576 | tf_op jit(solution)/shard_map/all_to_all | solution.py:143
Sparse Core Ops, SparseCore 0:
  11.0 33.8 reduce-scatter.2
  86.6 20.6 all-gather.4
  135.6 40.3 all-gather.6
  181.2 37.2 reduce-scatter.4
